TPU v7x, 32 devices: a whole 2x2x4 slice. The times are simulated.
32 devices in a mesh: groups: 2 (over x), gx: 16 (over z, y, core).
Axes of the slice: x: 2, y: 2, z: 4, core: 2. Of those that a mesh axis runs over, the one named last changes fastest.
Arguments:
- tokens: bfloat16 [768, 4608], P('groups', 'gx'), parts along dimension 0, may hold values from -6 to 6
- gate_weight: bfloat16 [16, 576, 9216], P('gx'), may hold values from -0.09375 to 0.09375
- up_weight: bfloat16 [16, 576, 9216], P('gx'), may hold values from -0.09375 to 0.09375
- down_weight: bfloat16 [16, 2304, 2304], P('gx'), may hold values from -0.046875 to 0.046875
Outputs:
- mixed: bfloat16 [768, 4608], P('groups', 'gx'), parts along dimension 0
There are 2 independent parts, one for each index of `groups`. A program takes and returns all parts, laid end to end along the dimension named above; an argument that names none is the same for every part. Nothing has to cross between parts.
All inputs are finite; a program needn't handle non-finite values.
Results may differ from a plain program's by a relative error of at most 0.015.
Values may be sent and summed in bfloat16 or wider, within the bound.
A program may use at most 128 MiB of HBM per device.

v0:
```python
import jax
import jax.numpy as jnp
from jax import lax
from jax.sharding import PartitionSpec as P

XS = 8


def from_partner(block, axis, bit):
    count = lax.axis_size(axis)
    route = []
    for low in range(count):
        high = low | 1 << bit
        if high != low and high < count:
            route += [(low, high), (high, low)]
    return lax.ppermute(block, axis, route)


def bit_clear(device_index, bit_number):
    return device_index >> bit_number & 1 == 0


def shards(tokens, gate_weight, up_weight, down_weight):
    gate_tile = gate_weight[0]
    up_tile = up_weight[0]
    down_tile = down_weight[0]
    axis_count = lax.axis_size("gx")
    column_groups = axis_count // XS
    low_bits = XS.bit_length() - 1
    high_bits = column_groups.bit_length() - 1
    device_index = lax.axis_index("gx")
    joined = tokens
    for high_step in range(high_bits):
        bit_number = low_bits + high_step
        partner_piece = from_partner(joined, "gx", bit_number)
        joined = jnp.where(
            bit_clear(device_index, bit_number),
            jnp.concatenate([joined, partner_piece], axis=1),
            jnp.concatenate([partner_piece, joined], axis=1),
        )
    gate_part = jnp.dot(joined, gate_tile, preferred_element_type=jnp.float32)
    up_part = jnp.dot(joined, up_tile, preferred_element_type=jnp.float32)
    stacked = jnp.stack([gate_part, up_part])
    for low_step in range(low_bits):
        bit_number = low_bits - 1 - low_step
        half_width = stacked.shape[2] // 2
        lower_half = stacked[:, :, :half_width]
        upper_half = stacked[:, :, half_width:]
        keep_lower = bit_clear(device_index, bit_number)
        outgoing = jnp.where(keep_lower, upper_half, lower_half)
        kept_half = jnp.where(keep_lower, lower_half, upper_half)
        stacked = kept_half + from_partner(outgoing.astype(jnp.bfloat16), "gx", bit_number).astype(
            outgoing.dtype
        )
    hidden = (jax.nn.gelu(stacked[0], approximate=True) * stacked[1]).astype(jnp.bfloat16)
    hidden_joined = hidden
    for high_step in range(high_bits):
        bit_number = low_bits + high_step
        partner_hidden = from_partner(hidden_joined, "gx", bit_number)
        hidden_joined = jnp.where(
            bit_clear(device_index, bit_number),
            jnp.concatenate([hidden_joined, partner_hidden], axis=1),
            jnp.concatenate([partner_hidden, hidden_joined], axis=1),
        )
    partial_value = jnp.dot(hidden_joined, down_tile, preferred_element_type=jnp.float32)
    for low_step in range(low_bits):
        bit_number = low_bits - 1 - low_step
        half_width = partial_value.shape[1] // 2
        lower_half = partial_value[:, :half_width]
        upper_half = partial_value[:, half_width:]
        keep_lower = bit_clear(device_index, bit_number)
        outgoing = jnp.where(keep_lower, upper_half, lower_half)
        kept_half = jnp.where(keep_lower, lower_half, upper_half)
        partial_value = kept_half + from_partner(
            outgoing.astype(jnp.bfloat16), "gx", bit_number
        ).astype(outgoing.dtype)
    return partial_value.astype(jnp.bfloat16)


def solution(mesh):
    placed = (P("groups", "gx"), P("gx", None, None), P("gx", None, None), P("gx", None, None))
    return jax.shard_map(
        shards, mesh=mesh, in_specs=placed, out_specs=P("groups", "gx"), check_vma=False
    )
```

profile of v0, /device:TPU:0, one launch (start us, length us, event | category | flops | bytes accessed | tf_op | source)
XLA Modules:
  0.0 400.2 jit_solution(16185231709463987360)
XLA Ops:
  0.0 4.1 %collective-permute-start = (bf16[384,288]{0,1:T(8,128)(2,1)}, bf16[384,288]{0,1:T(8,128)(2,1)S(1)}, u32[]{:S(2)}, u32[]{:S(2)}) collective-permute-start(bf16[384,288]{0,1:T(8,128)(2,1)} %param.4), channel_id=1, source_target_pairs={{0,8},{8,0},{1,9},{9,1},{2,10},{10,2},{3,11},{11,3},{4,12},{12,4},... | collective-permute-start | bytes 663560 | tf_op jit(solution)/shard_map/ppermute | solution.py:16
  4.1 0.0 copy-start.3
  4.1 10.4 %collective-permute-done = bf16[384,288]{0,1:T(8,128)(2,1)S(1)} collective-permute-done((bf16[384,288]{0,1:T(8,128)(2,1)}, bf16[384,288]{0,1:T(8,128)(2,1)S(1)}, u32[]{:S(2)}, u32[]{:S(2)}) %collective-permute-start) | collective-permute-done | bytes 221216 | tf_op jit(solution)/shard_map/ppermute | solution.py:16
  14.4 10.2 %convolution_bitcast_fusion = f32[1,384,9216]{2,1,0:T(8,128)S(1)} fusion(bf16[1,576,9216]{2,1,0:T(8,128)(2,1)} %param.6, bf16[384,288]{0,1:T(8,128)(2,1)S(1)} %collective-permute-done, bf16[384,288]{0,1:T(8,128)(2,1)} %param.4, pred[]{:T(512)S(6)} %eq.19), kind=kOutput, calls=%fused_computation.6 | convolution fusion | flops 4078854144 | bytes 25214976 | tf_op jit(solution)/shard_map/dot_general | solution.py:42
  24.6 0.0 copy-done.3
  24.7 0.0 copy-start
  24.7 12.6 %convolution_bitcast_fusion.1 = f32[1,384,9216]{2,1,0:T(8,128)S(1)} fusion(bf16[1,576,9216]{2,1,0:T(8,128)(2,1)} %param.5, bf16[384,288]{0,1:T(8,128)(2,1)S(1)} %collective-permute-done, bf16[384,288]{0,1:T(8,128)(2,1)S(1)} %copy-done.3, pred[]{:T(512)S(6)} %eq.19), kind=kOutput, calls=%fused_computation.7 | convolution fusion | flops 4078854144 | bytes 25214976 | tf_op jit(solution)/shard_map/dot_general | solution.py:41
  37.3 0.0 copy-done
  37.3 0.0 copy-start.1
  37.3 4.9 %select_convert_fusion = bf16[2,384,4608]{2,1,0:T(8,128)(2,1)} fusion(pred[]{:T(512)S(6)} %eq.18, f32[1,384,9216]{2,1,0:T(8,128)S(1)} %convolution_bitcast_fusion, f32[1,384,9216]{2,1,0:T(8,128)S(1)} %convolution_bitcast_fusion.1), kind=kLoop, calls=%fused_computation.5 | loop fusion | flops 31850496 | bytes 35389440 | tf_op jit(solution)/shard_map/convert_element_type | solution.py:52
  42.2 2.4 copy-done.1
  44.6 0.8 collective-permute-start.1
  45.4 153.0 %collective-permute-done.1 = bf16[2,384,4608]{2,1,0:T(8,128)(2,1)} collective-permute-done((bf16[2,384,4608]{2,1,0:T(8,128)(2,1)}, bf16[2,384,4608]{2,1,0:T(8,128)(2,1)}, u32[]{:S(2)}, u32[]{:S(2)}) %collective-permute-start.1) | collective-permute-done | bytes 7077920 | tf_op jit(solution)/shard_map/ppermute | solution.py:16
  198.4 12.2 %convert_add_fusion = f32[2,384,4608]{2,1,0:T(8,128)S(1)} fusion(bf16[2,384,4608]{2,1,0:T(8,128)(2,1)} %collective-permute-done.1, pred[]{:T(512)S(6)} %eq.18, f32[1,384,9216]{2,1,0:T(8,128)} %copy-done, f32[1,384,9216]{2,1,0:T(8,128)} %copy-done.1), kind=kLoop, calls=%fused_computation.4 | loop fusion | flops 17694720 | bytes 49545216 | tf_op jit(solution)/shard_map/add | solution.py:52
  210.6 0.0 copy-start.2
  210.7 5.0 %copy-done.2 = f32[2,384,4608]{2,1,0:T(8,128)} copy-done((f32[2,384,4608]{2,1,0:T(8,128)}, f32[2,384,4608]{2,1,0:T(8,128)S(1)}, u32[]{:S(2)}) %copy-start.2) | copy-done | bytes 14155800
  215.7 2.3 select_convert_fusion.1
  218.0 1.4 collective-permute-start.2
  219.4 75.7 %collective-permute-done.2 = bf16[2,384,2304]{2,1,0:T(8,128)(2,1)S(1)} collective-permute-done((bf16[2,384,2304]{2,1,0:T(8,128)(2,1)}, bf16[2,384,2304]{2,1,0:T(8,128)(2,1)S(1)}, u32[]{:S(2)}, u32[]{:S(2)}) %collective-permute-start.2) | collective-permute-done | bytes 3538976 | tf_op jit(solution)/shard_map/ppermute | solution.py:16
  295.1 8.9 %convert_add_fusion.1 = f32[2,384,2304]{2,1,0:T(8,128)} fusion(bf16[2,384,2304]{2,1,0:T(8,128)(2,1)S(1)} %collective-permute-done.2, f32[2,384,4608]{2,1,0:T(8,128)} %copy-done.2, pred[]{:T(512)S(6)} %eq.17), kind=kLoop, calls=%fused_computation.12 | loop fusion | flops 5308416 | bytes 24772608 | tf_op jit(solution)/shard_map/add | solution.py:52
  304.0 0.0 slice-start
  304.0 3.5 select_convert_fusion.2
  307.6 0.0 slice-start.1
  307.6 0.0 slice-start.2
  307.6 0.1 collective-permute-start.3
  307.7 3.7 collective-permute-done.3
  311.4 3.7 convert_add_fusion.2
  315.0 0.6 fusion.13
  315.7 4.2 %collective-permute-start.4 = (bf16[384,1152]{1,0:T(8,128)(2,1)S(1)}, bf16[384,1152]{1,0:T(8,128)(2,1)S(1)}, u32[]{:S(2)}, u32[]{:S(2)}) collective-permute-start(bf16[384,1152]{1,0:T(8,128)(2,1)S(1)} %fusion.13), channel_id=1, source_target_pairs={{0,8},{8,0},{1,9},{9,1},{2,10},{10,2},{3,11},{11,3},{4,12},{12,4},... | collective-permute-start | bytes 2654216 | tf_op jit(solution)/shard_map/ppermute | solution.py:16
  319.9 38.9 %collective-permute-done.4 = bf16[384,1152]{1,0:T(8,128)(2,1)S(1)} collective-permute-done((bf16[384,1152]{1,0:T(8,128)(2,1)S(1)}, bf16[384,1152]{1,0:T(8,128)(2,1)S(1)}, u32[]{:S(2)}, u32[]{:S(2)}) %collective-permute-start.4) | collective-permute-done | bytes 884768 | tf_op jit(solution)/shard_map/ppermute | solution.py:16
  358.8 0.0 slice-done
  358.8 0.0 slice-done.1
  358.8 0.0 slice-done.2
  358.8 4.4 %fusion.1 = f32[384,2304]{1,0:T(8,128)S(1)} fusion(bf16[1,2304,2304]{2,1,0:T(8,128)(2,1)S(1)} %bitcast.22, bf16[384,1152]{1,0:T(8,128)(2,1)S(1)} %collective-permute-done.4, bf16[384,1152]{1,0:T(8,128)(2,1)S(1)} %fusion.13, pred[]{:T(512)S(6)} %eq.19), kind=kOutput, calls=%fused_computation.8 | convolution fusion | flops 4084826112 | bytes 15925249 | tf_op jit(solution)/shard_map/dot_general | solution.py:65
  363.3 0.2 select_convert_fusion.3
  363.4 0.8 collective-permute-start.5
  364.2 20.4 %collective-permute-done.5 = bf16[384,1152]{1,0:T(8,128)(2,1)S(1)} collective-permute-done((bf16[384,1152]{1,0:T(8,128)(2,1)S(1)}, bf16[384,1152]{1,0:T(8,128)(2,1)S(1)}, u32[]{:S(2)}, u32[]{:S(2)}) %collective-permute-start.5) | collective-permute-done | bytes 884768 | tf_op jit(solution)/shard_map/ppermute | solution.py:16
  384.6 0.2 convert_add_fusion.3
  384.8 0.2 select_convert_fusion.4
  385.1 1.6 collective-permute-start.6
  386.6 10.3 %collective-permute-done.6 = bf16[384,576]{1,0:T(8,128)(2,1)S(1)} collective-permute-done((bf16[384,576]{1,0:T(8,128)(2,1)S(1)}, bf16[384,576]{1,0:T(8,128)(2,1)S(1)}, u32[]{:S(2)}, u32[]{:S(2)}) %collective-permute-start.6) | collective-permute-done | bytes 442400 | tf_op jit(solution)/shard_map/ppermute | solution.py:16
  397.0 0.3 convert_add_fusion.4
  397.3 0.2 select_convert_fusion.5
  397.5 0.1 collective-permute-start.7
  397.5 1.6 collective-permute-done.7
  399.1 0.2 add_convert_fusion
  399.3 0.8 copy.5
  (1 shorter events, 0.0 us)
Async XLA Ops:
  0.0 14.4 %collective-permute-start = (bf16[384,288]{0,1:T(8,128)(2,1)}, bf16[384,288]{0,1:T(8,128)(2,1)S(1)}, u32[]{:S(2)}, u32[]{:S(2)}) collective-permute-start(bf16[384,288]{0,1:T(8,128)(2,1)} %param.4), channel_id=1, source_target_pairs={{0,8},{8,0},{1,9},{9,1},{2,10},{10,2},{3,11},{11,3},{4,12},{12,4},... | collective-permute-start | bytes 663560 | tf_op jit(solution)/shard_map/ppermute | solution.py:16
  4.1 20.6 %copy-start.3 = (bf16[384,288]{0,1:T(8,128)(2,1)S(1)}, bf16[384,288]{0,1:T(8,128)(2,1)}, u32[]{:S(2)}) copy-start(bf16[384,288]{0,1:T(8,128)(2,1)} %param.4) | copy-start | bytes 663556
  24.7 12.6 %copy-start = (f32[1,384,9216]{2,1,0:T(8,128)}, f32[1,384,9216]{2,1,0:T(8,128)S(1)}, u32[]{:S(2)}) copy-start(f32[1,384,9216]{2,1,0:T(8,128)S(1)} %convolution_bitcast_fusion) | copy-start | bytes 42467332
  37.3 7.3 %copy-start.1 = (f32[1,384,9216]{2,1,0:T(8,128)}, f32[1,384,9216]{2,1,0:T(8,128)S(1)}, u32[]{:S(2)}) copy-start(f32[1,384,9216]{2,1,0:T(8,128)S(1)} %convolution_bitcast_fusion.1) | copy-start | bytes 42467332
  44.6 153.8 %collective-permute-start.1 = (bf16[2,384,4608]{2,1,0:T(8,128)(2,1)}, bf16[2,384,4608]{2,1,0:T(8,128)(2,1)}, u32[]{:S(2)}, u32[]{:S(2)}) collective-permute-start(bf16[2,384,4608]{2,1,0:T(8,128)(2,1)} %select_convert_fusion), channel_id=1, source_target_pairs={{0,4},{4,0},{1,5},{5,1},{2,6},{6,2},{3,7},{7,3},{8,12},{12,8},{9,1... | collective-permute-start | bytes 21233672 | tf_op jit(solution)/shard_map/ppermute | solution.py:16
  210.6 5.1 %copy-start.2 = (f32[2,384,4608]{2,1,0:T(8,128)}, f32[2,384,4608]{2,1,0:T(8,128)S(1)}, u32[]{:S(2)}) copy-start(f32[2,384,4608]{2,1,0:T(8,128)S(1)} %convert_add_fusion) | copy-start | bytes 42467332
  218.0 77.0 %collective-permute-start.2 = (bf16[2,384,2304]{2,1,0:T(8,128)(2,1)}, bf16[2,384,2304]{2,1,0:T(8,128)(2,1)S(1)}, u32[]{:S(2)}, u32[]{:S(2)}) collective-permute-start(bf16[2,384,2304]{2,1,0:T(8,128)(2,1)} %select_convert_fusion.1), channel_id=1, source_target_pairs={{0,2},{2,0},{1,3},{3,1},{4,6},{6,4},{5,7},{7,5},{8,10},{10,8},{9,1... | collective-permute-start | bytes 10616840 | tf_op jit(solution)/shard_map/ppermute | solution.py:16
  304.0 54.8 %slice-start = ((s8[10616832]{0:T(1024)(128)(4,1)}), s8[4194304]{0:T(1024)(128)(4,1)S(1)}, s32[]{:S(2)}) async-start(s8[10616832]{0:T(1024)(128)(4,1)} %bitcast.21), calls=%async_computation | async-start | bytes 8388608
  307.6 51.2 %slice-start.1 = ((s8[10616832]{0:T(1024)(128)(4,1)}), s8[4194304]{0:T(1024)(128)(4,1)S(1)}, s32[]{:S(2)}) async-start(s8[10616832]{0:T(1024)(128)(4,1)} %bitcast.21), calls=%async_computation.1 | async-start | bytes 8388608
  307.6 51.2 %slice-start.2 = ((s8[10616832]{0:T(1024)(128)(4,1)}), s8[2228224]{0:T(1024)(128)(4,1)S(1)}, s32[]{:S(2)}) async-start(s8[10616832]{0:T(1024)(128)(4,1)} %bitcast.21), calls=%async_computation.2 | async-start | bytes 4456448
  307.6 3.8 collective-permute-start.3
  315.7 43.1 %collective-permute-start.4 = (bf16[384,1152]{1,0:T(8,128)(2,1)S(1)}, bf16[384,1152]{1,0:T(8,128)(2,1)S(1)}, u32[]{:S(2)}, u32[]{:S(2)}) collective-permute-start(bf16[384,1152]{1,0:T(8,128)(2,1)S(1)} %fusion.13), channel_id=1, source_target_pairs={{0,8},{8,0},{1,9},{9,1},{2,10},{10,2},{3,11},{11,3},{4,12},{12,4},... | collective-permute-start | bytes 2654216 | tf_op jit(solution)/shard_map/ppermute | solution.py:16
  363.4 21.2 %collective-permute-start.5 = (bf16[384,1152]{1,0:T(8,128)(2,1)S(1)}, bf16[384,1152]{1,0:T(8,128)(2,1)S(1)}, u32[]{:S(2)}, u32[]{:S(2)}) collective-permute-start(bf16[384,1152]{1,0:T(8,128)(2,1)S(1)} %select_convert_fusion.3), channel_id=1, source_target_pairs={{0,4},{4,0},{1,5},{5,1},{2,6},{6,2},{3,7},{7,3},{8,12},{12,8},{9,1... | collective-permute-start | bytes 2654216 | tf_op jit(solution)/shard_map/ppermute | solution.py:16
  385.1 11.9 %collective-permute-start.6 = (bf16[384,576]{1,0:T(8,128)(2,1)S(1)}, bf16[384,576]{1,0:T(8,128)(2,1)S(1)}, u32[]{:S(2)}, u32[]{:S(2)}) collective-permute-start(bf16[384,576]{1,0:T(8,128)(2,1)S(1)} %select_convert_fusion.4), channel_id=1, source_target_pairs={{0,2},{2,0},{1,3},{3,1},{4,6},{6,4},{5,7},{7,5},{8,10},{10,8},{9,1... | collective-permute-start | bytes 1327112 | tf_op jit(solution)/shard_map/ppermute | solution.py:16
  397.5 1.6 collective-permute-start.7
where the time goes:
time: 400 us
  waiting for transfers between devices  314 us (78%)
  other arithmetic  37.5 us (9%)
  matrix products  27.2 us (7%)
  starting transfers between devices  13 us (3%)
  local copies, waits for them, and re-layouts  8.31 us (2%)
    ppermute x8, waiting for transfers between devices, from_partner(): return lax.ppermute(block, axis, route)  314 us
    add x5, other arithmetic, shards(): kept_half + from_partner(outgoing.astype(jnp.bfloat16), 'gx', bit_number)...  25.4 us
    ppermute x8, starting transfers between devices, from_partner(): return lax.ppermute(block, axis, route)  13 us
    dot_general x1, matrix products, shards(): gate_part = jnp.dot(joined, gate_tile, preferred_element_type=jnp.float32)  12.6 us
    convert_element_type x6, other arithmetic, shards(): outgoing.astype(jnp.bfloat16)  11.3 us
    dot_general x1, matrix products, shards(): up_part = jnp.dot(joined, up_tile, preferred_element_type=jnp.float32)  10.2 us
  transfers between devices with their start and end apart: 8, of which 8 were waited for; matrix products, arithmetic and copies ran while one was open for 0% of the time, Pallas kernels for 0%

commit v1 on v0

--- a/solution.py
+++ b/solution.py
@@ -1,9 +1,16 @@
 import jax
 import jax.numpy as jnp
 from jax import lax
+from jax.experimental import pallas as pl
+from jax.experimental.pallas import tpu as pltpu
 from jax.sharding import PartitionSpec as P
 
 XS = 8
+CHUNKS = 3
+Z_PARTS, ALL_PARTS = 1, 4
+VMEM_BYTES = 67043328
+MESH = pl.DeviceIdType.MESH
+DIAG, ZN, YN, OWN = 0, 1, 2, 3
 
 
 def from_partner(block, axis, bit):
@@ -20,7 +27,7 @@
     return device_index >> bit_number & 1 == 0
 
 
-def shards(tokens, gate_weight, up_weight, down_weight):
+def plain_shards(tokens, gate_weight, up_weight, down_weight):
     gate_tile = gate_weight[0]
     up_tile = up_weight[0]
     down_tile = down_weight[0]
@@ -41,8 +48,7 @@
     gate_part = jnp.dot(joined, gate_tile, preferred_element_type=jnp.float32)
     up_part = jnp.dot(joined, up_tile, preferred_element_type=jnp.float32)
     stacked = jnp.stack([gate_part, up_part])
-    for low_step in range(low_bits):
-        bit_number = low_bits - 1 - low_step
+    for bit_number in range(low_bits - 1, -1, -1):
         half_width = stacked.shape[2] // 2
         lower_half = stacked[:, :, :half_width]
         upper_half = stacked[:, :, half_width:]
@@ -63,8 +69,7 @@
             jnp.concatenate([partner_hidden, hidden_joined], axis=1),
         )
     partial_value = jnp.dot(hidden_joined, down_tile, preferred_element_type=jnp.float32)
-    for low_step in range(low_bits):
-        bit_number = low_bits - 1 - low_step
+    for bit_number in range(low_bits - 1, -1, -1):
         half_width = partial_value.shape[1] // 2
         lower_half = partial_value[:, :half_width]
         upper_half = partial_value[:, half_width:]
@@ -77,6 +82,383 @@
     return partial_value.astype(jnp.bfloat16)
 
 
+def tile_of(width):
+    for tiles in range(1, width // 128 + 1):
+        if width % tiles == 0 and (width // tiles) % 128 == 0 and width // tiles <= 512:
+            return width // tiles
+    return 128
+
+
+def gelu(v):
+    return 0.5 * v * (1.0 + jnp.tanh(0.7978845608 * (v + 0.044715 * (v * v * v))))
+
+
+def kernel(
+    tok, gate, up, down, out,
+    tok_in, joined, wts, wd, sib_out, sib_in, z1_out, y1_out, z2_out, y2_out,
+    z1_in, y1_in, z2_in, y2_in, keep_z, keep_y, keep_o, hid, hid_in,
+    acc, blocks, keep_d, dsib_out, dsib_in, dout, din,
+    tok_s, tok_r, w_sem, wd_sem, sib_s, sib_r, z1_s, z1_r, y1_s, y1_r,
+    z2_s, z2_r, y2_s, y2_r, hid_s, hid_r, dsib_s, dsib_r, dout_s, dout_r,
+):
+    bf16, f32 = jnp.bfloat16, jnp.float32
+    me = lax.axis_index("gx")
+    c, yb, zb, a = me % 2, (me // 2) % 2, (me // 4) % 2, me // 8
+    chunks = hid.shape[0]
+    rows = hid.shape[1]
+    feat = tok.shape[1]
+    width = hid.shape[2]
+    h0 = z1_out.shape[3]
+    col = tile_of(width)
+    ncol = width // col
+    to_c = me + 1 - 2 * c
+    to_y = me + 2 - 4 * yb
+    to_z = me + 4 - 8 * zb
+    to_d = me + 2 - 4 * yb + 4 - 8 * zb
+    to_a = me + 8 - 16 * a
+
+    def block_of(kind, core):
+        zz = 1 - zb if kind in (DIAG, ZN) else zb
+        yy = 1 - yb if kind in (DIAG, YN) else yb
+        return zz * 4 + yy * 2 + core
+
+    def remote(src, dst, ss, rs, target):
+        return pltpu.make_async_remote_copy(
+            src_ref=src, dst_ref=dst, send_sem=ss, recv_sem=rs,
+            device_id={"gx": target}, device_id_type=MESH,
+        )
+
+    def weight_copies(slot):
+        block = block_of(slot // 2, 1 - c if slot % 2 == 0 else c)
+        cols = pl.ds(pl.multiple_of(block * width, 128), width)
+        return [
+            pltpu.make_async_copy(w.at[0, :, cols], wts.at[i, slot], w_sem.at[i, slot])
+            for i, w in ((0, gate), (1, up))
+        ]
+
+    order = [2 * k for k in range(4)] + [2 * k + 1 for k in range(4)]
+    for slot in order:
+        for copy in weight_copies(slot):
+            copy.start()
+    down_copy = pltpu.make_async_copy(down.at[0], wd, wd_sem)
+    down_copy.start()
+
+    barrier = pltpu.get_barrier_semaphore()
+    for target in (to_c, to_y, to_z, to_d, to_a):
+        pl.semaphore_signal(barrier, inc=1, device_id={"gx": target}, device_id_type=MESH)
+    pl.semaphore_wait(barrier, 5)
+
+    def tok_copy(s):
+        r = pl.ds(s * rows, rows)
+        return remote(tok.at[r], tok_in.at[r], tok_s.at[s], tok_r.at[s], to_a)
+
+    for s in range(chunks):
+        tok_copy(s).start()
+
+    def join(s):
+        tok_copy(s).wait_recv()
+        r = pl.ds(s * rows, rows)
+
+        @pl.when(a == 0)
+        def _():
+            joined[r, 0:feat] = tok[r, :]
+            joined[r, feat:2 * feat] = tok_in[r, :]
+
+        @pl.when(a == 1)
+        def _():
+            joined[r, 0:feat] = tok_in[r, :]
+            joined[r, feat:2 * feat] = tok[r, :]
+
+    def each_tile(s, slot, body):
+        if s == 0:
+            for copy in weight_copies(slot):
+                copy.wait()
+        lhs = joined.at[pl.ds(s * rows, rows), :]
+
+        def step(t, carry):
+            g = t // ncol
+            cols = pl.ds(pl.multiple_of((t % ncol) * col, 128), col)
+            part = jnp.dot(lhs[...], wts[g, slot, :, cols], preferred_element_type=f32)
+            body(g, cols, part)
+            return carry
+
+        lax.fori_loop(0, 2 * ncol, step, 0)
+
+    def sib_copy(s, kind):
+        return remote(sib_out.at[kind], sib_in.at[s, kind], sib_s.at[s, kind], sib_r.at[s, kind], to_c)
+
+    def sibling(s, kind):
+        if s > 0:
+            sib_copy(s - 1, kind).wait_send()
+
+        def body(g, cols, part):
+            sib_out[kind, g, :, cols] = part.astype(bf16)
+
+        each_tile(s, 2 * kind, body)
+        sib_copy(s, kind).start()
+
+    def z1_copy(s, piece):
+        return remote(z1_out.at[s % 2, piece], z1_in.at[s, piece], z1_s.at[s, piece], z1_r.at[s, piece], to_z)
+
+    def y1_copy(s, piece):
+        return remote(y1_out.at[s % 2, piece], y1_in.at[s, piece], y1_s.at[s, piece], y1_r.at[s, piece], to_y)
+
+    def z2_copy(s):
+        return remote(z2_out.at[s % 2], z2_in.at[s], z2_s.at[s], z2_r.at[s], to_z)
+
+    def y2_copy(s):
+        return remote(y2_out.at[s % 2], y2_in.at[s], y2_s.at[s], y2_r.at[s], to_y)
+
+    def own(s, kind):
+        k = s % 2
+        if s >= 2 and kind in (DIAG, ZN):
+            z1_copy(s - 2, kind).wait_send()
+        if s >= 2 and kind in (DIAG, YN):
+            y1_copy(s - 2, 0 if kind == DIAG else 1).wait_send()
+        sib_copy(s, kind).wait_recv()
+
+        def body(g, cols, part):
+            total = part + sib_in[s, kind, g, :, cols].astype(f32)
+            if kind == DIAG:
+                z1_out[k, 0, g, :, cols] = total[:h0].astype(bf16)
+                y1_out[k, 0, g, :, cols] = total[h0:].astype(bf16)
+            elif kind == ZN:
+                z1_out[k, 1, g, :, cols] = total[:h0].astype(bf16)
+                keep_z[k, g, :, cols] = total[h0:]
+            elif kind == YN:
+                y1_out[k, 1, g, :, cols] = total[h0:].astype(bf16)
+                keep_y[k, g, :, cols] = total[:h0]
+            else:
+                keep_o[g, :, cols] = total
+
+        each_tile(s, 2 * kind + 1, body)
+        if kind == DIAG:
+            z1_copy(s, 0).start()
+            y1_copy(s, 0).start()
+        elif kind == ZN:
+            z1_copy(s, 1).start()
+        elif kind == YN:
+            y1_copy(s, 1).start()
+
+    def loop_cols(body):
+        def step(t, carry):
+            body(t // ncol, pl.ds(pl.multiple_of((t % ncol) * col, 128), col))
+            return carry
+
+        lax.fori_loop(0, 2 * ncol, step, 0)
+
+    def relay(s):
+        k = s % 2
+        if s >= 2:
+            y2_copy(s - 2).wait_send()
+            z2_copy(s - 2).wait_send()
+        z1_copy(s, 0).wait_recv()
+
+        def to_y2(g, cols):
+            y2_out[k, g, :, cols] = (keep_y[k, g, :, cols] + z1_in[s, 0, g, :, cols].astype(f32)).astype(bf16)
+
+        loop_cols(to_y2)
+        y2_copy(s).start()
+        y1_copy(s, 0).wait_recv()
+
+        def to_z2(g, cols):
+            z2_out[k, g, :, cols] = (keep_z[k, g, :, cols] + y1_in[s, 0, g, :, cols].astype(f32)).astype(bf16)
+
+        loop_cols(to_z2)
+        z2_copy(s).start()
+
+    def hid_copy(s):
+        return remote(hid.at[s], hid_in.at[s], hid_s.at[s], hid_r.at[s], to_a)
+
+    def finish(s):
+        own(s, OWN)
+        z1_copy(s, 1).wait_recv()
+        y1_copy(s, 1).wait_recv()
+        y2_copy(s).wait_recv()
+        z2_copy(s).wait_recv()
+
+        def step(t, carry):
+            cols = pl.ds(pl.multiple_of(t * col, 128), col)
+            for r, first, second in (
+                (slice(0, h0), z1_in.at[s, 1], y2_in.at[s]),
+                (slice(h0, rows), y1_in.at[s, 1], z2_in.at[s]),
+            ):
+                g, u = (
+                    keep_o[i, r, cols] + first[i, :, cols].astype(f32) + second[i, :, cols].astype(f32)
+                    for i in (0, 1)
+                )
+                hid[s, r, cols] = (gelu(g) * u).astype(bf16)
+            return carry
+
+        lax.fori_loop(0, ncol, step, 0)
+        hid_copy(s).start()
+
+    full = acc.shape[1]
+    dcol = tile_of(full)
+    dwidth = blocks.shape[2]
+
+    def dsib_copy(s, kind):
+        return remote(dsib_out.at[s, kind], dsib_in.at[s, kind], dsib_s.at[s, kind], dsib_r.at[s, kind], to_c)
+
+    def dout_copy(s, kind):
+        target = (to_d, to_z, to_y)[kind]
+        return remote(dout.at[s, kind], din.at[s, kind], dout_s.at[s, kind], dout_r.at[s, kind], target)
+
+    def project(s):
+        if s == 0:
+            down_copy.wait()
+        first = pl.ds(pl.multiple_of(a * width, 128), width)
+        second = pl.ds(pl.multiple_of((1 - a) * width, 128), width)
+
+        def own_half(t, carry):
+            cols = pl.ds(pl.multiple_of(t * dcol, 128), dcol)
+            acc[:, cols] = jnp.dot(hid[s], wd[first, cols], preferred_element_type=f32)
+            return carry
+
+        lax.fori_loop(0, full // dcol, own_half, 0)
+        hid_copy(s).wait_recv()
+
+        def other_half(t, carry):
+            cols = pl.ds(pl.multiple_of(t * dcol, 128), dcol)
+            acc[:, cols] += jnp.dot(hid_in[s], wd[second, cols], preferred_element_type=f32)
+            return carry
+
+        lax.fori_loop(0, full // dcol, other_half, 0)
+        for b in range(XS):
+            blocks[b] = acc[:, b * dwidth:(b + 1) * dwidth]
+        for kind in range(4):
+            dsib_out[s, kind] = blocks[block_of(kind, 1 - c)].astype(bf16)
+            dsib_copy(s, kind).start()
+
+    def spread(s):
+        for kind in range(4):
+            dsib_copy(s, kind).wait_recv()
+            total = blocks[block_of(kind, c)] + dsib_in[s, kind].astype(f32)
+            if kind == OWN:
+                keep_d[s] = total
+            else:
+                dout[s, kind] = total.astype(bf16)
+                dout_copy(s, kind).start()
+
+    join(0)
+    for kind in range(4):
+        sibling(0, kind)
+    for s in range(chunks):
+        if s + 1 < chunks:
+            join(s + 1)
+        for kind in range(3):
+            own(s, kind)
+            if s + 1 < chunks:
+                sibling(s + 1, kind)
+        if s + 1 < chunks:
+            sibling(s + 1, OWN)
+        if s > 0:
+            relay(s - 1)
+    if chunks > 1:
+        finish(0)
+    relay(chunks - 1)
+    if chunks == 1:
+        finish(0)
+    for s in range(chunks):
+        project(s)
+        if s + 1 < chunks:
+            finish(s + 1)
+        spread(s)
+    for s in range(chunks):
+        total = keep_d[s]
+        for kind in range(3):
+            dout_copy(s, kind).wait_recv()
+            total = total + din[s, kind].astype(f32)
+        out[pl.ds(s * rows, rows), :] = total.astype(bf16)
+
+    for s in range(chunks):
+        tok_copy(s).wait_send()
+        hid_copy(s).wait_send()
+        for kind in range(4):
+            if s == chunks - 1:
+                sib_copy(s, kind).wait_send()
+            dsib_copy(s, kind).wait_send()
+        for kind in range(3):
+            dout_copy(s, kind).wait_send()
+        if s >= chunks - 2:
+            for piece in range(2):
+                z1_copy(s, piece).wait_send()
+                y1_copy(s, piece).wait_send()
+            z2_copy(s).wait_send()
+            y2_copy(s).wait_send()
+
+
+def fused(chunks, tokens, gate_weight, up_weight, down_weight):
+    count, feat = tokens.shape
+    depth, half = gate_weight.shape[1:]
+    deep, full = down_weight.shape[1:]
+    rows, width, dwidth = count // chunks, half // XS, full // XS
+    h0 = rows // 16 * Z_PARTS // ALL_PARTS * 16
+    h1 = rows - h0
+    bf16, f32 = jnp.bfloat16, jnp.float32
+    v = pltpu.VMEM
+    pair = min(chunks, 2)
+    buffers = [
+        v((count, feat), bf16),
+        v((count, 2 * feat), bf16),
+        v((2, XS, depth, width), bf16),
+        v((deep, full), bf16),
+        v((4, 2, rows, width), bf16),
+        v((chunks, 4, 2, rows, width), bf16),
+        v((pair, 2, 2, h0, width), bf16),
+        v((pair, 2, 2, h1, width), bf16),
+        v((pair, 2, h1, width), bf16),
+        v((pair, 2, h0, width), bf16),
+        v((chunks, 2, 2, h0, width), bf16),
+        v((chunks, 2, 2, h1, width), bf16),
+        v((chunks, 2, h1, width), bf16),
+        v((chunks, 2, h0, width), bf16),
+        v((pair, 2, h1, width), f32),
+        v((pair, 2, h0, width), f32),
+        v((2, rows, width), f32),
+        v((chunks, rows, width), bf16),
+        v((chunks, rows, width), bf16),
+        v((rows, full), f32),
+        v((XS, rows, dwidth), f32),
+        v((chunks, rows, dwidth), f32),
+        v((chunks, 4, rows, dwidth), bf16),
+        v((chunks, 4, rows, dwidth), bf16),
+        v((chunks, 3, rows, dwidth), bf16),
+        v((chunks, 3, rows, dwidth), bf16),
+    ]
+    sem = pltpu.SemaphoreType.DMA
+    s = chunks
+    shapes = [(s,), (s,), (2, XS), None, (s, 4), (s, 4), (s, 2), (s, 2), (s, 2), (s, 2)]
+    shapes += [(s,)] * 6 + [(s, 4), (s, 4), (s, 3), (s, 3)]
+    sems = [sem if shape is None else sem(shape) for shape in shapes]
+    vmem = pl.BlockSpec(memory_space=pltpu.VMEM)
+    hbm = pl.BlockSpec(memory_space=pl.ANY)
+    return pl.pallas_call(
+        kernel,
+        out_shape=jax.ShapeDtypeStruct((count, dwidth), bf16),
+        in_specs=[vmem, hbm, hbm, hbm],
+        out_specs=vmem,
+        scratch_shapes=buffers + sems,
+        compiler_params=pltpu.CompilerParams(
+            collective_id=0, has_side_effects=True, vmem_limit_bytes=VMEM_BYTES
+        ),
+    )(tokens, gate_weight, up_weight, down_weight)
+
+
+def shards(tokens, gate_weight, up_weight, down_weight):
+    width = gate_weight.shape[2] // XS
+    suits = (
+        lax.axis_size("gx") == 2 * XS
+        and width % 128 == 0
+        and down_weight.shape[2] % 128 == 0
+        and tokens.shape[0] % (CHUNKS * 64) == 0
+        and tokens.shape[1] % 16 == 0
+    )
+    if suits:
+        return fused(CHUNKS, tokens, gate_weight, up_weight, down_weight)
+    return plain_shards(tokens, gate_weight, up_weight, down_weight)
+
+
 def solution(mesh):
     placed = (P("groups", "gx"), P("gx", None, None), P("gx", None, None), P("gx", None, None))
     return jax.shard_map(

time: 400 us -> 126 us (0.32)
  waiting for transfers between devices: 314 us -> 0 us
  Pallas kernels: 0 us -> 122 us
  other arithmetic: 37.5 us -> 0 us
  matrix products: 27.2 us -> 0 us
  starting transfers between devices: 13 us -> 0 us
  local copies, waits for them, and re-layouts: 8.31 us -> 3.61 us
    ppermute x8 -> x0, waiting for transfers between devices: 314 us -> none  [from_partner(): return lax.ppermute(block, axis, route)]
    pallas_call x0 -> x1, Pallas kernels: none -> 122 us  [fused(): pl.pallas_call(kernel, out_shape=jax.ShapeDtypeStruct((count, dwidth), bf...]
    dot_general x3 -> x0, matrix products: 27.2 us -> none  [the longest x1 12.6 us: shards(): gate_part = jnp.dot(joined, gate_tile, preferred_element_type=jnp.float32)]
    add x5 -> x0, other arithmetic: 25.4 us -> none  [shards(): kept_half + from_partner(outgoing.astype(jnp.bfloat16), 'gx', bit_number)...]
    ppermute x8 -> x0, starting transfers between devices: 13 us -> none  [from_partner(): return lax.ppermute(block, axis, route)]
    convert_element_type x8 -> x0, other arithmetic: 12.1 us -> none  [the longest x6 11.3 us: shards(): outgoing.astype(jnp.bfloat16)]
    unnamed x14 -> x1, local copies, waits for them, and re-layouts: 7.47 us -> 1.81 us
  transfers between devices with their start and end apart: 8 -> 0, of which waited for: 8 -> 0; matrix products, arithmetic and copies ran while one was open for 0% -> 0% of each run, Pallas kernels for 0% -> 0%
where the time goes in v1:
time: 126 us
  Pallas kernels  122 us (97%)
  local copies, waits for them, and re-layouts  3.61 us (3%)
    pallas_call x1, Pallas kernels, fused(): pl.pallas_call(kernel, out_shape=jax.ShapeDtypeStruct((count, dwidth), bf...  122 us

profile of v1, /device:TPU:0, one launch (start us, length us, event | category | flops | bytes accessed | tf_op | source)
XLA Modules:
  0.0 125.9 jit_solution(16278202650448616589)
XLA Ops:
  0.0 1.8 %copy.5.tok = bf16[384,288]{1,0:T(8,128)(2,1)} copy(bf16[384,288]{0,1:T(8,128)(2,1)} %param.4) | data formatting | bytes 442368 | tf_op args[0]
  1.8 122.3 %shard_map.46 = bf16[384,288]{1,0:T(8,128)(2,1)} custom-call(bf16[384,288]{1,0:T(8,128)(2,1)} %copy.5.tok, bf16[1,576,9216]{2,1,0:T(8,128)(2,1)} %gate.1, bf16[1,576,9216]{2,1,0:T(8,128)(2,1)} %up.1, bf16[1,2304,2304]{2,1,0:T(8,128)(2,1)} %down.1), custom_call_target="tpu_custom_call" | custom-call | tf_op jit(solution)/shard_map/pallas_call | solution.py:436
  124.1 1.8 %copy.6 = bf16[384,288]{0,1:T(8,128)(2,1)} copy(bf16[384,288]{1,0:T(8,128)(2,1)} %shard_map.46) | data formatting | bytes 442368 | tf_op jit(solution)/shard_map/pallas_call | solution.py:436

commit v2 on v1

--- a/solution.py
+++ b/solution.py
@@ -7,7 +7,7 @@
 
 XS = 8
 CHUNKS = 3
-Z_PARTS, ALL_PARTS = 1, 4
+Z_PARTS, ALL_PARTS = 3, 8
 VMEM_BYTES = 67043328
 MESH = pl.DeviceIdType.MESH
 DIAG, ZN, YN, OWN = 0, 1, 2, 3
@@ -84,7 +84,7 @@
 
 def tile_of(width):
     for tiles in range(1, width // 128 + 1):
-        if width % tiles == 0 and (width // tiles) % 128 == 0 and width // tiles <= 512:
+        if width % tiles == 0 and (width // tiles) % 128 == 0 and width // tiles <= 2304:
             return width // tiles
     return 128
 
@@ -344,25 +344,22 @@
     for kind in range(4):
         sibling(0, kind)
     for s in range(chunks):
+        for kind in range(3):
+            own(s, kind)
         if s + 1 < chunks:
             join(s + 1)
-        for kind in range(3):
-            own(s, kind)
-            if s + 1 < chunks:
+            for kind in range(4):
                 sibling(s + 1, kind)
-        if s + 1 < chunks:
-            sibling(s + 1, OWN)
         if s > 0:
-            relay(s - 1)
-    if chunks > 1:
-        finish(0)
-    relay(chunks - 1)
-    if chunks == 1:
-        finish(0)
+            finish(s - 1)
+        relay(s)
     for s in range(chunks):
-        project(s)
-        if s + 1 < chunks:
-            finish(s + 1)
+        if s < chunks - 1:
+            project(s)
+        if s == max(chunks - 2, 0):
+            finish(chunks - 1)
+        if s == chunks - 1:
+            project(s)
         spread(s)
     for s in range(chunks):
         total = keep_d[s]

time: 126 us -> 113 us (0.90)
  Pallas kernels: 122 us -> 109 us
    pallas_call x1, Pallas kernels: 122 us -> 109 us  [fused(): pl.pallas_call(kernel, out_shape=jax.ShapeDtypeStruct((count, dwidth), bf...]
where the time goes in v2:
time: 113 us
  Pallas kernels  109 us (96%)
  local copies, waits for them, and re-layouts  3.61 us (3%)
    pallas_call x1, Pallas kernels, fused(): pl.pallas_call(kernel, out_shape=jax.ShapeDtypeStruct((count, dwidth), bf...  109 us

profile of v2, /device:TPU:0, one launch (start us, length us, event | category | flops | bytes accessed | tf_op | source)
XLA Modules:
  0.0 113.0 jit_solution(3607257849968028829)
XLA Ops:
  0.0 1.8 %copy.5.tok = bf16[384,288]{1,0:T(8,128)(2,1)} copy(bf16[384,288]{0,1:T(8,128)(2,1)} %param.4) | data formatting | bytes 442368 | tf_op args[0]
  1.8 109.4 %shard_map.46 = bf16[384,288]{1,0:T(8,128)(2,1)} custom-call(bf16[384,288]{1,0:T(8,128)(2,1)} %copy.5.tok, bf16[1,576,9216]{2,1,0:T(8,128)(2,1)} %gate.1, bf16[1,576,9216]{2,1,0:T(8,128)(2,1)} %up.1, bf16[1,2304,2304]{2,1,0:T(8,128)(2,1)} %down.1), custom_call_target="tpu_custom_call" | custom-call | tf_op jit(solution)/shard_map/pallas_call | solution.py:433
  111.2 1.8 %copy.6 = bf16[384,288]{0,1:T(8,128)(2,1)} copy(bf16[384,288]{1,0:T(8,128)(2,1)} %shard_map.46) | data formatting | bytes 442368 | tf_op jit(solution)/shard_map/pallas_call | solution.py:433
